TPU v7x, 32 devices: a whole 2x2x4 slice. The times are simulated.
32 devices in a mesh: row: 4 (over y, x), col: 8 (over z, core).
Axes of the slice: x: 2, y: 2, z: 4, core: 2. Of those that a mesh axis runs over, the one named last changes fastest.
Arguments:
- trial: bfloat16 [2, 512, 2048], P(None, 'row', 'col'), may hold values from -6 to 6
- val_energy: float32 [512], P('row'), may hold values from -1 to 0
- cond_energy: float32 [2048], P('col'), may hold values from 0.5 to 2
- val_orbitals: bfloat16 [512, 20480], P('col', 'row'), may hold values from -0.25 to 0.25
- cond_orbitals: bfloat16 [2048, 20480], P('row', 'col'), may hold values from -0.125 to 0.125
- screening: bfloat16 [20480, 20480], P('row', 'col'), may hold values from -0.29882812 to 0.29882812
Outputs:
- applied: float32 [2, 512, 2048], P(None, 'row', 'col')
All inputs are finite; a program needn't handle non-finite values.
Results may differ from a plain program's by a relative error of at most 0.0028.
Values may be sent and summed in bfloat16 or wider, within the bound.
No kernel may reach another device: no remote copies, remote signals or barrier semaphores. Data moves between devices by JAX's collectives and lax.ppermute only.
A program may use at most 128 MiB of HBM per device.

v0:
```python
import jax
import jax.numpy as jnp
from jax import lax
from jax.sharding import PartitionSpec as P


def local(trial, val_energy, cond_energy, val_orbitals, cond_orbitals, screening):
    full_trial = lax.all_gather(trial, "col", axis=2, tiled=True)
    cond_full = lax.all_gather(cond_orbitals, "row", axis=0, tiled=True)
    val_full = lax.all_gather(val_orbitals, "col", axis=0, tiled=True)
    encoded = jnp.einsum(
        "bvc,cn->bvn", full_trial, cond_full, preferred_element_type=jnp.float32
    ).astype(jnp.bfloat16)
    scr_float = screening.astype(jnp.float32)

    def decode_part(enc_part):
        val_rows = val_full
        moments = jnp.einsum(
            "vm,bvn->bmn",
            val_rows,
            lax.all_gather(enc_part, "row", axis=1, tiled=True),
            preferred_element_type=jnp.float32,
        )
        screened = (scr_float[None] * moments).astype(jnp.bfloat16)
        val_rows = val_full
        half = lax.psum_scatter(
            jnp.einsum("vm,bmn->vbn", val_rows, screened, preferred_element_type=jnp.float32),
            "row",
            scatter_dimension=0,
            tiled=True,
        ).astype(jnp.bfloat16)
        partial_kernel = jnp.einsum(
            "vbn,cn->bvc", half, cond_full, preferred_element_type=jnp.float32
        )
        return lax.psum_scatter(partial_kernel, "col", scatter_dimension=2, tiled=True)

    pieces = [decode_part(encoded[b : b + 1]) for b in range(trial.shape[0])]
    kernel = jnp.concatenate(pieces, axis=0)
    gaps = cond_energy[None, None, :] - val_energy[None, :, None]
    return gaps * trial.astype(jnp.float32) + kernel


def solution(mesh):
    placed = (
        P(None, "row", "col"),
        P("row"),
        P("col"),
        P("col", "row"),
        P("row", "col"),
        P("row", "col"),
    )
    return jax.shard_map(
        local, mesh=mesh, in_specs=placed, out_specs=P(None, "row", "col"), check_vma=False
    )
```

profile of v0, /device:TPU:0, one launch (start us, length us, event | category | flops | bytes accessed | tf_op | source)
XLA Modules:
  0.0 484.8 jit_solution(12320645691943452132)
XLA Ops:
  6.5 0.7 all-gather.6.cloned.1.call-update
  7.3 0.7 all-gather.8.cloned.1.call-update
  8.1 0.7 all-gather.12.cloned.1.call-update
  8.8 26.8 %all-gather.6.cloned.1.call-done = bf16[2,128,2048]{2,1,0:T(8,128)(2,1)} async-done(((bf16[2,128,256]{2,1,0:T(8,128)(2,1)}), bf16[2,128,2048]{2,1,0:T(8,128)(2,1)}) %all-gather.6.cloned.1.call-update) | async-done | bytes 1048592 | tf_op jit(solution)/shard_map/all_gather | solution.py:8
  35.6 105.6 %all-gather.8.cloned.1.call-done = bf16[2048,2560]{1,0:T(8,128)(2,1)} async-done(((bf16[512,2560]{1,0:T(8,128)(2,1)}), bf16[2048,2560]{1,0:T(8,128)(2,1)}) %all-gather.8.cloned.1.call-update) | async-done | bytes 10485776 | tf_op jit(solution)/shard_map/all_gather | solution.py:9
  141.1 7.2 %fusion.14 = bf16[2,128,2560]{2,1,0:T(8,128)(2,1)S(1)} fusion(bf16[2,128,2048]{2,1,0:T(8,128)(2,1)} %all-gather.6.cloned.1.call-done, bf16[2048,2560]{1,0:T(8,128)(2,1)} %all-gather.8.cloned.1.call-done), kind=kOutput, calls=%fused_computation.12 | convolution fusion | flops 2685009920 | bytes 12845056 | tf_op jit(solution)/shard_map/bvc,cn->bvn/dot_general | solution.py:11
  148.3 1.1 fusion.25
  149.5 0.0 all-gather.14.cloned.1.call-start
  149.5 34.4 %copy.7 = bf16[5120,2560]{0,1:T(8,128)(2,1)} copy(bf16[5120,2560]{1,0:T(8,128)(2,1)} %param.11) | data formatting | bytes 52428800 | tf_op args[5]
  184.0 14.8 %all-gather.12.cloned.1.call-done = bf16[512,5120]{1,0:T(8,128)(2,1)} async-done(((bf16[64,5120]{1,0:T(8,128)(2,1)}), bf16[512,5120]{1,0:T(8,128)(2,1)}) %all-gather.12.cloned.1.call-update) | async-done | bytes 5242896 | tf_op jit(solution)/shard_map/all_gather | solution.py:10
  198.8 40.0 %all-gather.10.cloned.1.call-done = bf16[1,512,2560]{2,1,0:T(8,128)(2,1)} async-done(((bf16[1,128,2560]{2,1,0:T(8,128)(2,1)}), bf16[1,512,2560]{2,1,0:T(8,128)(2,1)}) %all-gather.10.cloned.1.call-update) | async-done | bytes 2621456 | tf_op jit(solution)/shard_map/all_gather | solution.py:21
  238.8 37.3 %fusion.8 = f32[512,1,2560]{0,2,1:T(8,128)} fusion(bf16[512,5120]{1,0:T(8,128)(2,1)} %all-gather.12.cloned.1.call-done, bf16[5120,2560]{0,1:T(8,128)(2,1)} %copy.7, bf16[1,512,2560]{2,1,0:T(8,128)(2,1)} %all-gather.10.cloned.1.call-done), kind=kOutput, calls=%fused_computation.10 | convolution fusion | flops 26882867200 | bytes 39321600 | tf_op jit(solution)/shard_map/vm,bmn->vbn/dot_general | solution.py:27
  276.1 0.2 reduce-scatter.9.cloned.1.call-start
  276.3 3.7 all-gather.14.cloned.1.call-done
  280.0 37.3 %fusion.11 = f32[512,1,2560]{0,2,1:T(8,128)} fusion(bf16[512,5120]{1,0:T(8,128)(2,1)} %all-gather.12.cloned.1.call-done, bf16[5120,2560]{0,1:T(8,128)(2,1)} %copy.7, bf16[1,512,2560]{2,1,0:T(8,128)(2,1)} %all-gather.14.cloned.1.call-done), kind=kOutput, calls=%fused_computation.11 | convolution fusion | flops 26882867200 | bytes 39321600 | tf_op jit(solution)/shard_map/vm,bmn->vbn/dot_general | solution.py:27
  317.3 26.9 %reduce-scatter.5.cloned.1.call-done = f32[128,1,2560]{0,2,1:T(8,128)} async-done(((f32[512,1,2560]{0,2,1:T(8,128)}), f32[128,1,2560]{0,2,1:T(8,128)}) %reduce-scatter.5.cloned.1.call-update) | async-done | bytes 1310736 | tf_op jit(solution)/shard_map/reduce_scatter | solution.py:26
  344.2 8.9 %convolution_bitcast_fusion.1 = f32[1,128,2048]{2,1,0:T(8,128)} fusion(bf16[2048,2560]{1,0:T(8,128)(2,1)} %all-gather.8.cloned.1.call-done, f32[128,1,2560]{0,2,1:T(8,128)} %reduce-scatter.5.cloned.1.call-done), kind=kOutput, calls=%fused_computation.16 | convolution fusion | flops 1342504960 | bytes 12845056 | tf_op jit(solution)/shard_map/vbn,cn->bvc/dot_general | solution.py:32
  353.2 0.0 reduce-scatter.11.cloned.1.call-start
  353.2 55.3 %reduce-scatter.9.cloned.1.call-done = f32[128,1,2560]{0,2,1:T(8,128)} async-done(((f32[512,1,2560]{0,2,1:T(8,128)}), f32[128,1,2560]{0,2,1:T(8,128)}) %reduce-scatter.9.cloned.1.call-update) | async-done | bytes 1310736 | tf_op jit(solution)/shard_map/reduce_scatter | solution.py:26
  408.6 9.0 %convolution_bitcast_fusion = f32[1,128,2048]{2,1,0:T(8,128)} fusion(bf16[2048,2560]{1,0:T(8,128)(2,1)} %all-gather.8.cloned.1.call-done, f32[128,1,2560]{0,2,1:T(8,128)} %reduce-scatter.9.cloned.1.call-done), kind=kOutput, calls=%fused_computation.15 | convolution fusion | flops 1342504960 | bytes 12845056 | tf_op jit(solution)/shard_map/vbn,cn->bvc/dot_general | solution.py:32
  417.5 0.1 broadcast_subtract_fusion
  417.6 25.8 %reduce-scatter.7.cloned.1.call-done = f32[1,128,256]{2,1,0:T(8,128)} async-done(((f32[1,128,2048]{2,1,0:T(8,128)}), f32[1,128,256]{2,1,0:T(8,128)}) %reduce-scatter.7.cloned.1.call-update) | async-done | bytes 131088 | tf_op jit(solution)/shard_map/reduce_scatter | solution.py:35
  443.5 33.1 %reduce-scatter.11.cloned.1.call-done = f32[1,128,256]{2,1,0:T(8,128)} async-done(((f32[1,128,2048]{2,1,0:T(8,128)}), f32[1,128,256]{2,1,0:T(8,128)}) %reduce-scatter.11.cloned.1.call-update) | async-done | bytes 131088 | tf_op jit(solution)/shard_map/reduce_scatter | solution.py:35
  476.5 1.7 maximum_add_fusion
  (18 shorter events, 0.3 us)
Async XLA Ops:
  6.5 29.0 %all-gather.6.cloned.1.call-start = ((), (), s32[]{:S(2)}) async-start(), calls=%async_computation.4 | async-start | bytes 1179648 | tf_op jit(solution)/shard_map/all_gather | solution.py:8
  7.3 133.9 %all-gather.8.cloned.1.call-start = ((), (), s32[]{:S(2)}) async-start(), calls=%async_computation.5 | async-start | bytes 13107200 | tf_op jit(solution)/shard_map/all_gather | solution.py:9
  8.0 190.8 %all-gather.12.cloned.1.call-start = ((), (), s32[]{:S(2)}) async-start(), calls=%async_computation.7 | async-start | bytes 5898240 | tf_op jit(solution)/shard_map/all_gather | solution.py:10
  8.7 230.0 %all-gather.10.cloned.1.call-start = ((), (), s32[]{:S(2)}) async-start(), calls=%async_computation.6 | async-start | bytes 3276800 | tf_op jit(solution)/shard_map/all_gather | solution.py:21
  149.5 130.5 %all-gather.14.cloned.1.call-start = ((), (), s32[]{:S(2)}) async-start(), calls=%async_computation.10 | async-start | bytes 3276800 | tf_op jit(solution)/shard_map/all_gather | solution.py:21
  183.9 160.3 %reduce-scatter.5.cloned.1.call-start = ((), (), s32[]{:S(2)}) async-start(), calls=%async_computation.8 | async-start | bytes 6553600 | tf_op jit(solution)/shard_map/reduce_scatter | solution.py:26
  276.1 132.5 %reduce-scatter.9.cloned.1.call-start = ((), (), s32[]{:S(2)}) async-start(), calls=%async_computation.11 | async-start | bytes 6553600 | tf_op jit(solution)/shard_map/reduce_scatter | solution.py:26
  317.3 126.2 %reduce-scatter.7.cloned.1.call-start = ((), (), s32[]{:S(2)}) async-start(), calls=%async_computation.9 | async-start | bytes 1179648 | tf_op jit(solution)/shard_map/reduce_scatter | solution.py:35
  353.1 64.4 %copy-start.1 = (f32[256]{0:T(256)S(1)}, f32[256]{0:T(256)}, u32[]{:S(2)}) copy-start(f32[256]{0:T(256)} %param.8) | copy-start | bytes 3076
  353.1 64.4 %copy-start.2 = (f32[128]{0:T(128)S(1)}, f32[128]{0:T(128)}, u32[]{:S(2)}) copy-start(f32[128]{0:T(128)} %param.7) | copy-start | bytes 1540
  353.1 123.4 %copy-start = (bf16[2,128,256]{2,1,0:T(8,128)(2,1)S(1)}, bf16[2,128,256]{2,1,0:T(8,128)(2,1)}, u32[]{:S(2)}) copy-start(bf16[2,128,256]{2,1,0:T(8,128)(2,1)} %param.6) | copy-start | bytes 393220
  353.2 123.4 %reduce-scatter.11.cloned.1.call-start = ((), (), s32[]{:S(2)}) async-start(), calls=%async_computation.12 | async-start | bytes 1179648 | tf_op jit(solution)/shard_map/reduce_scatter | solution.py:35
Sparse Core Ops, SparseCore 0:
  8.9 26.5 all-gather.5
  37.4 103.6 all-gather.7
  142.8 55.9 all-gather.11
  200.5 38.2 all-gather.9
  240.5 39.4 all-gather.13
  282.8 61.3 reduce-scatter.4
  347.2 61.3 reduce-scatter.8
  410.8 32.5 reduce-scatter.6
  445.7 30.7 reduce-scatter.10
where the time goes:
time: 486 us; the launch traced here: 485 us
  waiting for transfers between devices  334 us (69%)
  matrix products  99.5 us (20%)
  local copies, waits for them, and re-layouts  35.6 us (7%)
  between operations  13.3 us (3%)
    all_gather x1, waiting for transfers between devices, local(): cond_full = lax.all_gather(cond_orbitals, 'row', axis=0, tiled=True)  106 us
    reduce_scatter x2, waiting for transfers between devices, decode_part(): lax.psum_scatter(jnp.einsum('vm,bmn->vbn', val_rows, screened, preferred_...  82.2 us
    dot_general x2, matrix products, decode_part(): jnp.einsum('vm,bmn->vbn', val_rows, screened, preferred_element_type=jnp....  74.5 us
    reduce_scatter x2, waiting for transfers between devices, decode_part(): lax.psum_scatter(partial_kernel, 'col', scatter_dimension=2, tiled=True)  58.9 us
    all_gather x2, waiting for transfers between devices, decode_part(): lax.all_gather(enc_part, 'row', axis=1, tiled=True)  43.7 us
    unnamed x7, local copies, waits for them, and re-layouts  34.4 us
    all_gather x1, waiting for transfers between devices, local(): full_trial = lax.all_gather(trial, 'col', axis=2, tiled=True)  26.8 us
    dot_general x2, matrix products, decode_part(): jnp.einsum('vbn,cn->bvc', half, cond_full, preferred_element_type=jnp.flo...  17.8 us
  transfers between devices with their start and end apart: 9, of which 9 were waited for; matrix products, arithmetic and copies ran while one was open for 28% of the time, Pallas kernels for 0%

commit v1 on v0

--- a/solution.py
+++ b/solution.py
@@ -5,11 +5,38 @@
 
 
 def local(trial, val_energy, cond_energy, val_orbitals, cond_orbitals, screening):
-    full_trial = lax.all_gather(trial, "col", axis=2, tiled=True)
+
+    def see_the_fields(frame, on_dim, xs):
+        part_now = lax.axis_size("col")
+        n_now, mat_out, newest = (part_now, lax.axis_index("col"), frame.shape[on_dim])
+        lanes = tuple(((s, (s + 1) % n_now) for s in range(n_now)))
+        found = tuple(((s, (s - 1) % n_now) for s in range(n_now)))
+        x_now = n_now // 2
+        right_arr = h_now = frame
+        upper = xs(frame, mat_out * newest)
+        i = 1
+        while i < x_now + 1:
+            right_arr = lax.ppermute(right_arr, axis_name="col", perm=lanes)
+            if i < n_now - x_now:
+                h_now = lax.ppermute(h_now, "col", perm=found)
+                piece_now = xs(h_now, (mat_out + i) % n_now * newest)
+                upper = upper + piece_now
+            v_now = xs(right_arr, (mat_out - i) % n_now * newest)
+            upper = upper + v_now
+            i = i + 1
+        return upper
+
     cond_full = lax.all_gather(cond_orbitals, "row", axis=0, tiled=True)
     val_full = lax.all_gather(val_orbitals, "col", axis=0, tiled=True)
-    encoded = jnp.einsum(
-        "bvc,cn->bvn", full_trial, cond_full, preferred_element_type=jnp.float32
+    encoded = see_the_fields(
+        trial,
+        on_dim=2,
+        xs=lambda own_block, at: jnp.einsum(
+            "bvc,cn->bvn",
+            own_block,
+            lax.dynamic_slice_in_dim(cond_full, at, own_block.shape[2], axis=0),
+            preferred_element_type=jnp.float32,
+        ),
     ).astype(jnp.bfloat16)
     scr_float = screening.astype(jnp.float32)
 

time: 486 us -> 463 us (0.953)
  waiting for transfers between devices: 334 us -> 299 us
  starting transfers between devices: 0.51 us -> 12.3 us
    all_gather x1 -> x0, waiting for transfers between devices: 26.8 us -> none  [local(): full_trial = lax.all_gather(trial, 'col', axis=2, tiled=True)]
    all_gather x1, waiting for transfers between devices: 106 us -> 86.2 us  [local(): cond_full = lax.all_gather(cond_orbitals, 'row', axis=0, tiled=True)]
    ppermute x0 -> x7, starting transfers between devices: none -> 11.8 us  [the longest x3 11.3 us: see_the_fields(): h_now = lax.ppermute(h_now, 'col', perm=found)]
    ppermute x0 -> x7, waiting for transfers between devices: none -> 8.83 us  [the longest x4 8.73 us: see_the_fields(): right_arr = lax.ppermute(right_arr, axis_name='col', perm=lanes)]
    unnamed x7 -> x10, local copies, waits for them, and re-layouts: 34.4 us -> 37.2 us
  transfers between devices with their start and end apart: 9 -> 15, of which waited for: 9 -> 12; matrix products, arithmetic and copies ran while one was open for 28% -> 28% of each run, Pallas kernels for 0% -> 0%
where the time goes in v1:
time: 463 us; the launch traced here: 462 us
  waiting for transfers between devices  299 us (65%)
  matrix products  97 us (21%)
  local copies, waits for them, and re-layouts  38.3 us (8%)
  between operations  13.6 us (3%)
  starting transfers between devices  12.3 us (3%)
    all_gather x1, waiting for transfers between devices, local(): cond_full = lax.all_gather(cond_orbitals, 'row', axis=0, tiled=True)  86.2 us
    reduce_scatter x2, waiting for transfers between devices, decode_part(): lax.psum_scatter(jnp.einsum('vm,bmn->vbn', val_rows, screened, preferred_...  84.3 us
    dot_general x2, matrix products, decode_part(): jnp.einsum('vm,bmn->vbn', val_rows, screened, preferred_element_type=jnp....  74 us
    reduce_scatter x2, waiting for transfers between devices, decode_part(): lax.psum_scatter(partial_kernel, 'col', scatter_dimension=2, tiled=True)  60.9 us
    all_gather x2, waiting for transfers between devices, decode_part(): lax.all_gather(enc_part, 'row', axis=1, tiled=True)  43.8 us
    unnamed x10, local copies, waits for them, and re-layouts  37.2 us
    all_gather x1, waiting for transfers between devices, local(): val_full = lax.all_gather(val_orbitals, 'col', axis=0, tiled=True)  14.5 us
    dot_general x2, matrix products, decode_part(): jnp.einsum('vbn,cn->bvc', half, cond_full, preferred_element_type=jnp.flo...  13.9 us
  transfers between devices with their start and end apart: 15, of which 12 were waited for; matrix products, arithmetic and copies ran while one was open for 28% of the time, Pallas kernels for 0%

profile of v1, /device:TPU:0, one launch (start us, length us, event | category | flops | bytes accessed | tf_op | source)
XLA Modules:
  0.0 462.4 jit_solution(18012152841609825693)
XLA Ops:
  6.5 4.4 copy.8
  12.3 4.1 collective-permute-start
  16.4 2.7 collective-permute-done.1
  19.1 3.5 collective-permute-start.2
  22.7 3.3 collective-permute-done.3
  26.1 3.7 collective-permute-start.4
  29.8 2.7 collective-permute-done.5
  32.5 86.2 %all-gather.5.cloned.1.call-done = bf16[2048,2560]{0,1:T(8,128)(2,1)} async-done(((bf16[512,2560]{0,1:T(8,128)(2,1)}), bf16[2048,2560]{0,1:T(8,128)(2,1)}) %all-gather.5.cloned.1.call-update) | async-done | bytes 10485776 | tf_op jit(solution)/shard_map/all_gather | solution.py:29
  118.7 1.8 fusion.29
  120.5 2.0 fusion.24
  122.5 2.4 convolution_add_fusion.4
  129.5 32.3 %copy.7 = bf16[5120,2560]{0,1:T(8,128)(2,1)} copy(bf16[5120,2560]{1,0:T(8,128)(2,1)} %param.11) | data formatting | bytes 52428800 | tf_op args[5]
  161.8 14.5 %all-gather.9.cloned.1.call-done = bf16[512,5120]{1,0:T(8,128)(2,1)} async-done(((bf16[64,5120]{1,0:T(8,128)(2,1)}), bf16[512,5120]{1,0:T(8,128)(2,1)}) %all-gather.9.cloned.1.call-update) | async-done | bytes 5242896 | tf_op jit(solution)/shard_map/all_gather | solution.py:30
  176.3 40.0 %all-gather.7.cloned.1.call-done = bf16[1,512,2560]{1,2,0:T(8,128)(2,1)} async-done(((bf16[1,128,2560]{1,2,0:T(8,128)(2,1)}), bf16[1,512,2560]{1,2,0:T(8,128)(2,1)}) %all-gather.7.cloned.1.call-update) | async-done | bytes 2621456 | tf_op jit(solution)/shard_map/all_gather | solution.py:48
  216.3 37.0 %fusion.6 = f32[512,1,2560]{0,2,1:T(8,128)} fusion(bf16[512,5120]{1,0:T(8,128)(2,1)} %all-gather.9.cloned.1.call-done, bf16[5120,2560]{0,1:T(8,128)(2,1)} %copy.7, bf16[1,512,2560]{1,2,0:T(8,128)(2,1)} %all-gather.7.cloned.1.call-done), kind=kOutput, calls=%fused_computation.8 | convolution fusion | flops 26882867200 | bytes 39321600 | tf_op jit(solution)/shard_map/vm,bmn->vbn/dot_general | solution.py:54
  253.6 3.8 all-gather.11.cloned.1.call-done
  257.4 37.0 %fusion.9 = f32[512,1,2560]{0,2,1:T(8,128)} fusion(bf16[512,5120]{1,0:T(8,128)(2,1)} %all-gather.9.cloned.1.call-done, bf16[5120,2560]{0,1:T(8,128)(2,1)} %copy.7, bf16[1,512,2560]{1,2,0:T(8,128)(2,1)} %all-gather.11.cloned.1.call-done), kind=kOutput, calls=%fused_computation.9 | convolution fusion | flops 26882867200 | bytes 39321600 | tf_op jit(solution)/shard_map/vm,bmn->vbn/dot_general | solution.py:54
  294.5 27.1 %reduce-scatter.5.cloned.1.call-done = f32[128,1,2560]{0,2,1:T(8,128)} async-done(((f32[512,1,2560]{0,2,1:T(8,128)}), f32[128,1,2560]{0,2,1:T(8,128)}) %reduce-scatter.5.cloned.1.call-update) | async-done | bytes 1310736 | tf_op jit(solution)/shard_map/reduce_scatter | solution.py:53
  321.6 6.9 %convolution_bitcast_fusion.1 = f32[1,128,2048]{2,1,0:T(8,128)} fusion(bf16[2048,2560]{0,1:T(8,128)(2,1)} %all-gather.5.cloned.1.call-done, f32[128,1,2560]{0,2,1:T(8,128)} %reduce-scatter.5.cloned.1.call-done), kind=kOutput, calls=%fused_computation.22 | convolution fusion | flops 1342504960 | bytes 12845056 | tf_op jit(solution)/shard_map/vbn,cn->bvc/dot_general | solution.py:59
  328.6 57.2 %reduce-scatter.9.cloned.1.call-done = f32[128,1,2560]{0,2,1:T(8,128)} async-done(((f32[512,1,2560]{0,2,1:T(8,128)}), f32[128,1,2560]{0,2,1:T(8,128)}) %reduce-scatter.9.cloned.1.call-update) | async-done | bytes 1310736 | tf_op jit(solution)/shard_map/reduce_scatter | solution.py:53
  385.8 7.0 %convolution_bitcast_fusion = f32[1,128,2048]{2,1,0:T(8,128)} fusion(bf16[2048,2560]{0,1:T(8,128)(2,1)} %all-gather.5.cloned.1.call-done, f32[128,1,2560]{0,2,1:T(8,128)} %reduce-scatter.9.cloned.1.call-done), kind=kOutput, calls=%fused_computation.21 | convolution fusion | flops 1342504960 | bytes 12845056 | tf_op jit(solution)/shard_map/vbn,cn->bvc/dot_general | solution.py:59
  392.9 27.8 %reduce-scatter.7.cloned.1.call-done = f32[1,128,256]{2,1,0:T(8,128)} async-done(((f32[1,128,2048]{2,1,0:T(8,128)}), f32[1,128,256]{2,1,0:T(8,128)}) %reduce-scatter.7.cloned.1.call-update) | async-done | bytes 131088 | tf_op jit(solution)/shard_map/reduce_scatter | solution.py:62
  420.7 33.1 %reduce-scatter.11.cloned.1.call-done = f32[1,128,256]{2,1,0:T(8,128)} async-done(((f32[1,128,2048]{2,1,0:T(8,128)}), f32[1,128,256]{2,1,0:T(8,128)}) %reduce-scatter.11.cloned.1.call-update) | async-done | bytes 131088 | tf_op jit(solution)/shard_map/reduce_scatter | solution.py:62
  453.8 1.7 maximum_add_fusion
  (39 shorter events, 6.5 us)
Async XLA Ops:
  6.5 112.1 %all-gather.5.cloned.1.call-start = ((), (), s32[]{:S(2)}) async-start(), calls=%async_computation.4 | async-start | bytes 13107200 | tf_op jit(solution)/shard_map/all_gather | solution.py:29
  10.9 0.9 copy-start.1
  11.0 165.3 %all-gather.9.cloned.1.call-start = ((), (), s32[]{:S(2)}) async-start(), calls=%async_computation.6 | async-start | bytes 5898240 | tf_op jit(solution)/shard_map/all_gather | solution.py:30
  11.7 204.6 %all-gather.7.cloned.1.call-start = ((), (), s32[]{:S(2)}) async-start(), calls=%async_computation.5 | async-start | bytes 3276800 | tf_op jit(solution)/shard_map/all_gather | solution.py:48
  11.9 7.3 %collective-permute-start.1 = (bf16[2,128,256]{2,1,0:T(8,128)(2,1)S(1)}, bf16[2,128,256]{2,1,0:T(8,128)(2,1)S(1)}, u32[]{:S(2)}, u32[]{:S(2)}) collective-permute-start(bf16[2,128,256]{2,1,0:T(8,128)(2,1)S(1)} %copy-done.1), channel_id=1, source_target_pairs={{0,1},{1,2},{2,3},{3,4},{4,5},{5,6},{6,7},{7,0},{8,9},{9,10},{10,1... | collective-permute-start | bytes 393224 | tf_op jit(solution)/shard_map/ppermute | solution.py:19
  12.3 6.8 %collective-permute-start = (bf16[2,128,256]{2,1,0:T(8,128)(2,1)S(1)}, bf16[2,128,256]{2,1,0:T(8,128)(2,1)S(1)}, u32[]{:S(2)}, u32[]{:S(2)}) collective-permute-start(bf16[2,128,256]{2,1,0:T(8,128)(2,1)S(1)} %copy-done.1), channel_id=1, source_target_pairs={{0,7},{1,0},{2,1},{3,2},{4,3},{5,4},{6,5},{7,6},{8,15},{9,8},{10,9... | collective-permute-start | bytes 393224 | tf_op jit(solution)/shard_map/ppermute | solution.py:21
  19.1 6.9 %collective-permute-start.3 = (bf16[2,128,256]{2,1,0:T(8,128)(2,1)S(1)}, bf16[2,128,256]{2,1,0:T(8,128)(2,1)S(1)}, u32[]{:S(2)}, u32[]{:S(2)}) collective-permute-start(bf16[2,128,256]{2,1,0:T(8,128)(2,1)S(1)} %collective-permute-done.1), channel_id=1, source_target_pairs={{0,1},{1,2},{2,3},{3,4},{4,5},{5,6},{6,7},{7,0},{8,9},{9,10},{10,1... | collective-permute-start | bytes 393224 | tf_op jit(solution)/shard_map/ppermute | solution.py:19
  19.1 7.0 %collective-permute-start.2 = (bf16[2,128,256]{2,1,0:T(8,128)(2,1)S(1)}, bf16[2,128,256]{2,1,0:T(8,128)(2,1)S(1)}, u32[]{:S(2)}, u32[]{:S(2)}) collective-permute-start(bf16[2,128,256]{2,1,0:T(8,128)(2,1)S(1)} %collective-permute-done), channel_id=1, source_target_pairs={{0,7},{1,0},{2,1},{3,2},{4,3},{5,4},{6,5},{7,6},{8,15},{9,8},{10,9... | collective-permute-start | bytes 393224 | tf_op jit(solution)/shard_map/ppermute | solution.py:21
  26.0 6.5 %collective-permute-start.5 = (bf16[2,128,256]{2,1,0:T(8,128)(2,1)S(1)}, bf16[2,128,256]{2,1,0:T(8,128)(2,1)S(1)}, u32[]{:S(2)}, u32[]{:S(2)}) collective-permute-start(bf16[2,128,256]{2,1,0:T(8,128)(2,1)S(1)} %collective-permute-done.3), channel_id=1, source_target_pairs={{0,1},{1,2},{2,3},{3,4},{4,5},{5,6},{6,7},{7,0},{8,9},{9,10},{10,1... | collective-permute-start | bytes 393224 | tf_op jit(solution)/shard_map/ppermute | solution.py:19
  26.1 101.0 %collective-permute-start.4 = (bf16[2,128,256]{2,1,0:T(8,128)(2,1)S(1)}, bf16[2,128,256]{2,1,0:T(8,128)(2,1)S(1)}, u32[]{:S(2)}, u32[]{:S(2)}) collective-permute-start(bf16[2,128,256]{2,1,0:T(8,128)(2,1)S(1)} %collective-permute-done.2), channel_id=1, source_target_pairs={{0,7},{1,0},{2,1},{3,2},{4,3},{5,4},{6,5},{7,6},{8,15},{9,8},{10,9... | collective-permute-start | bytes 393224 | tf_op jit(solution)/shard_map/ppermute | solution.py:21
  32.5 95.2 %collective-permute-start.6 = (bf16[2,128,256]{2,1,0:T(8,128)(2,1)S(1)}, bf16[2,128,256]{2,1,0:T(8,128)(2,1)S(1)}, u32[]{:S(2)}, u32[]{:S(2)}) collective-permute-start(bf16[2,128,256]{2,1,0:T(8,128)(2,1)S(1)} %collective-permute-done.5), channel_id=1, source_target_pairs={{0,1},{1,2},{2,3},{3,4},{4,5},{5,6},{6,7},{7,0},{8,9},{9,10},{10,1... | collective-permute-start | bytes 393224 | tf_op jit(solution)/shard_map/ppermute | solution.py:19
  120.5 4.8 %copy-start = (bf16[2048,2560]{0,1:T(8,128)(2,1)S(1)}, bf16[2048,2560]{0,1:T(8,128)(2,1)}, u32[]{:S(2)}) copy-start(bf16[2048,2560]{0,1:T(8,128)(2,1)} %all-gather.5.cloned.1.call-done) | copy-start | bytes 31457284
  129.4 128.0 %all-gather.11.cloned.1.call-start = ((), (), s32[]{:S(2)}) async-start(), calls=%async_computation.9 | async-start | bytes 3276800 | tf_op jit(solution)/shard_map/all_gather | solution.py:48
  161.8 159.8 %reduce-scatter.5.cloned.1.call-start = ((), (), s32[]{:S(2)}) async-start(), calls=%async_computation.7 | async-start | bytes 6553600 | tf_op jit(solution)/shard_map/reduce_scatter | solution.py:53
  253.4 132.4 %reduce-scatter.9.cloned.1.call-start = ((), (), s32[]{:S(2)}) async-start(), calls=%async_computation.10 | async-start | bytes 6553600 | tf_op jit(solution)/shard_map/reduce_scatter | solution.py:53
  294.4 126.3 %reduce-scatter.7.cloned.1.call-start = ((), (), s32[]{:S(2)}) async-start(), calls=%async_computation.8 | async-start | bytes 1179648 | tf_op jit(solution)/shard_map/reduce_scatter | solution.py:62
  328.6 64.2 %copy-start.2 = (f32[256]{0:T(256)S(1)}, f32[256]{0:T(256)}, u32[]{:S(2)}) copy-start(f32[256]{0:T(256)} %param.8) | copy-start | bytes 3076
  328.6 64.2 %copy-start.3 = (f32[128]{0:T(128)S(1)}, f32[128]{0:T(128)}, u32[]{:S(2)}) copy-start(f32[128]{0:T(128)} %param.7) | copy-start | bytes 1540
  328.6 125.2 %reduce-scatter.11.cloned.1.call-start = ((), (), s32[]{:S(2)}) async-start(), calls=%async_computation.11 | async-start | bytes 1179648 | tf_op jit(solution)/shard_map/reduce_scatter | solution.py:62
Sparse Core Ops, SparseCore 0:
  11.1 107.5 all-gather.4
  120.3 55.9 all-gather.8
  178.1 38.1 all-gather.6
  218.0 39.3 all-gather.10
  260.2 61.3 reduce-scatter.4
  324.4 61.3 reduce-scatter.8
  388.1 32.6 reduce-scatter.6
  423.0 30.7 reduce-scatter.10
